TPU v7x, 32 devices: a whole 2x2x4 slice. The times are simulated.
32 devices in a mesh: ep: 4 (over z), fsdp: 8 (over y, x, core).
Axes of the slice: x: 2, y: 2, z: 4, core: 2. Of those that a mesh axis runs over, the one named last changes fastest.
Arguments:
- train_gate: float32 [64, 2048, 1408], P('ep', 'fsdp'), may hold values from -0.1875 to 0.1875
- train_up: float32 [64, 2048, 1408], P('ep', 'fsdp'), may hold values from -0.1875 to 0.1875
- train_down: float32 [64, 1408, 2048], P('ep', None, 'fsdp'), may hold values from -0.21875 to 0.21875
- router_weight: float32 [2048, 64], P('fsdp', 'ep'), may hold values from -0.125 to 0.125
- router_gain: float32 [2048], P('fsdp'), may hold values from 0.25 to 1.75
Outputs:
- ready_gate: bfloat16 [64, 2048, 1408], P('ep', None, 'fsdp')
- ready_up: bfloat16 [64, 2048, 1408], P('ep', None, 'fsdp')
- ready_down: bfloat16 [64, 1408, 2048], P('ep', 'fsdp')
- scale_gate: float32 [64, 1408], P('ep', 'fsdp')
- scale_up: float32 [64, 1408], P('ep', 'fsdp')
- scale_down: float32 [64, 1408], P('ep', 'fsdp')
- serve_router: bfloat16 [2048, 64], replicated
All inputs are finite; a program needn't handle non-finite values.
Results may differ from a plain program's by a relative error of at most 0.001.
Values may be sent and summed in bfloat16 or wider, within the bound.
A program may use at most 192 MiB of HBM per device.

v0:
```python
import jax
import jax.numpy as jnp
from jax import lax
from jax.sharding import PartitionSpec as P


def body(train_gate, train_up, train_down, router_weight, router_gain):
    total_gate, total_up, total_down = lax.psum(
        (
            jnp.sum(train_gate * train_gate, axis=1),
            jnp.sum(train_up * train_up, axis=1),
            jnp.sum(train_down * train_down, axis=2),
        ),
        "fsdp",
    )
    scale_gate = jnp.sqrt(total_gate)
    scale_up = jnp.sqrt(total_up)
    scale_down = jnp.sqrt(total_down)
    narrow_gate, narrow_up, narrow_down = (
        (train_gate / jnp.expand_dims(scale_gate, 1)).astype(jnp.bfloat16),
        (train_up / jnp.expand_dims(scale_up, 1)).astype(jnp.bfloat16),
        (train_down / jnp.expand_dims(scale_down, 2)).astype(jnp.bfloat16),
    )
    ready_gate, ready_up = (
        lax.all_to_all(narrow_gate, "fsdp", split_axis=2, concat_axis=1, tiled=True),
        lax.all_to_all(narrow_up, "fsdp", split_axis=2, concat_axis=1, tiled=True),
    )
    ready_down = lax.all_to_all(narrow_down, "fsdp", split_axis=1, concat_axis=2, tiled=True)
    scale_gate = lax.dynamic_slice_in_dim(
        scale_gate, lax.axis_index("fsdp") * ready_gate.shape[2], ready_gate.shape[2], axis=1
    )
    scale_up = lax.dynamic_slice_in_dim(
        scale_up, lax.axis_index("fsdp") * ready_up.shape[2], ready_up.shape[2], axis=1
    )
    scale_down = lax.dynamic_slice_in_dim(
        scale_down, lax.axis_index("fsdp") * ready_down.shape[1], ready_down.shape[1], axis=1
    )
    part_router = (router_weight * router_gain[:, None]).astype(jnp.bfloat16)
    row_router = lax.all_gather(part_router, "fsdp", axis=0, tiled=True)
    serve_router = lax.all_gather(row_router, "ep", axis=1, tiled=True)
    return (ready_gate, ready_up, ready_down, scale_gate, scale_up, scale_down, serve_router)


def solution(mesh):
    return jax.shard_map(
        body,
        mesh=mesh,
        in_specs=(
            P("ep", "fsdp", None),
            P("ep", "fsdp", None),
            P("ep", None, "fsdp"),
            P("fsdp", "ep"),
            P("fsdp"),
        ),
        out_specs=(
            P("ep", None, "fsdp"),
            P("ep", None, "fsdp"),
            P("ep", "fsdp", None),
            P("ep", "fsdp"),
            P("ep", "fsdp"),
            P("ep", "fsdp"),
            P(),
        ),
        check_vma=False,
    )
```

profile of v0, /device:TPU:0, one launch (start us, length us, event | category | flops | bytes accessed | tf_op | source)
XLA Modules:
  0.0 618.1 jit_solution(2208627624309375978)
XLA Ops:
  7.2 0.0 all-reduce.3.cloned.1.call-start
  7.2 0.0 copy-start
  7.2 9.2 %multiply_reduce_fusion = f32[16,1408]{1,0:T(8,128)} fusion(f32[16,1408,256]{2,1,0:T(8,128)} %param.7), kind=kLoop, calls=%fused_computation.2 | loop fusion | flops 11511808 | bytes 23158784 | tf_op jit(solution)/shard_map/reduce_sum | solution.py:12
  16.4 5.0 copy-done
  21.4 11.0 %multiply_reduce_fusion.1 = (f32[16,1408]{1,0:T(8,128)}, f32[16,1408]{1,0:T(8,128)}) fusion(f32[16,256,1408]{2,1,0:T(8,128)S(1)} %copy-done, f32[16,256,1408]{2,1,0:T(8,128)} %param.5), kind=kLoop, calls=%fused_computation.4 | loop fusion | flops 23023616 | bytes 46317568 | tf_op jit(solution)/shard_map/reduce_sum | solution.py:11
  32.5 0.0 all-reduce.3.cloned.1.call-update
  32.5 23.7 %copy.28 = f32[16,256,1408]{1,0,2:T(8,128)} copy(f32[16,256,1408]{2,1,0:T(8,128)} %param.6) | data formatting | bytes 46137344 | tf_op args[1]
  56.2 32.6 %all-reduce.3.cloned.1.call-done = (f32[16,1408]{1,0:T(8,128)}, f32[16,1408]{1,0:T(8,128)}, f32[16,1408]{1,0:T(8,128)}) async-done(((f32[16,1408]{1,0:T(8,128)}, f32[16,1408]{1,0:T(8,128)}, f32[16,1408]{1,0:T(8,128)}), (f32[16,1408]{1,0:T(8,128)}, f32[16,1408]{1,0:T(8,128)}, f32[16,1408]{1,0:T(8,128)})) %all-reduce.3.cloned.1.call-update) | async-done | bytes 270352 | tf_op jit(solution)/shard_map/psum | solution.py:8
  88.8 0.9 sqrt.10
  89.7 0.3 copy.27
  90.0 14.2 %divide_convert_fusion = bf16[16,256,1408]{1,0,2:T(8,128)(2,1)} fusion(f32[16,256,1408]{1,0,2:T(8,128)} %copy.28, f32[16,1408]{0,1:T(8,128)S(1)} %copy.27), kind=kLoop, calls=%fused_computation.3 | loop fusion | flops 11534336 | bytes 34693120 | tf_op jit(solution)/shard_map/convert_element_type | solution.py:21
  104.2 5.2 all-to-all-start.1
  109.5 0.0 copy-start.2
  109.5 23.7 %copy.24 = f32[16,256,1408]{1,0,2:T(8,128)} copy(f32[16,256,1408]{2,1,0:T(8,128)} %param.5) | data formatting | bytes 46137344 | tf_op args[0]
  133.2 0.0 copy-done.2
  133.2 0.3 copy.23
  133.5 0.0 copy-start.1
  133.5 14.2 %divide_convert_fusion.1 = bf16[16,256,1408]{1,0,2:T(8,128)(2,1)} fusion(f32[16,256,1408]{1,0,2:T(8,128)} %copy.24, f32[16,1408]{0,1:T(8,128)S(1)} %copy.23), kind=kLoop, calls=%fused_computation.5 | loop fusion | flops 11534336 | bytes 34693120 | tf_op jit(solution)/shard_map/convert_element_type | solution.py:20
  147.7 89.5 %all-to-all-done.1 = bf16[16,256,1408]{1,0,2:T(8,128)(2,1)} async-done(((bf16[16,256,1408]{1,0,2:T(8,128)(2,1)}), bf16[16,256,1408]{1,0,2:T(8,128)(2,1)}, u32[]{:S(2)}, u32[]{:S(2)}) %all-to-all-start.1) | async-done | bytes 11534368 | tf_op jit(solution)/shard_map/all_to_all | solution.py:26
  237.2 5.3 all-to-all-start
  242.5 0.0 copy-done.1
  242.5 0.3 copy.31
  242.8 0.0 copy-start.3
  242.8 0.0 copy-start.4
  242.8 32.6 %fusion = bf16[16,1408,256]{2,0,1:T(8,128)(2,1)} fusion(f32[16,1408,256]{2,1,0:T(8,128)} %param.7, f32[16,1408]{0,1:T(8,128)S(1)} %copy.31), kind=kLoop, calls=%fused_computation.1 | loop fusion | flops 11534336 | bytes 34693120 | tf_op jit(solution)/shard_map/convert_element_type | solution.py:22
  275.4 94.8 %all-to-all-done = bf16[16,256,1408]{1,0,2:T(8,128)(2,1)} async-done(((bf16[16,256,1408]{1,0,2:T(8,128)(2,1)}), bf16[16,256,1408]{1,0,2:T(8,128)(2,1)}, u32[]{:S(2)}, u32[]{:S(2)}) %all-to-all-start) | async-done | bytes 11534368 | tf_op jit(solution)/shard_map/all_to_all | solution.py:25
  370.2 5.3 all-to-all-start.2
  375.5 0.0 copy-done.3
  375.5 0.0 copy-done.4
  375.5 130.9 %all_gather.6 = bf16[2048,16]{0,1:T(8,128)(2,1)S(1)} all-gather(bf16[256,16]{0,1:T(8,128)(2,1)S(1)} %multiply_convert_fusion), channel_id=1, replica_groups=mesh['ep'=4,'fsdp'=8] {'fsdp'}, dimensions={0}, use_global_device_ids=true | all-gather | bytes 73728 | tf_op jit(solution)/shard_map/all_gather | solution.py:39
  506.4 14.2 %all_gather.7 = bf16[2048,64]{0,1:T(8,128)(2,1)S(1)} all-gather(bf16[2048,16]{0,1:T(8,128)(2,1)S(1)} %all_gather.6), channel_id=1, replica_groups=mesh['ep'=4,'fsdp'=8] {'ep'}, dimensions={1}, use_global_device_ids=true | all-gather | bytes 327680 | tf_op jit(solution)/shard_map/all_gather | solution.py:40
  520.6 0.7 constant_dynamic-slice_fusion
  521.3 0.7 constant_dynamic-slice_fusion.1
  522.0 0.7 constant_dynamic-slice_fusion.2
  522.6 11.3 %copy.30 = bf16[16,8,256,176]{2,1,3,0:T(8,128)(2,1)} copy(bf16[16,8,256,176]{2,0,3,1:T(8,128)(2,1)} %bitcast.5) | data formatting | bytes 23068672 | tf_op jit(solution)/shard_map/all_to_all | solution.py:26
  534.0 18.0 %all_to_all.46 = bf16[16,2048,176]{1,2,0:T(8,128)(2,1)} reshape(bf16[16,8,256,176]{2,1,3,0:T(8,128)(2,1)} %copy.30) | data formatting | bytes 23068672 | tf_op jit(solution)/shard_map/all_to_all | solution.py:26
  551.9 11.3 %copy.26 = bf16[16,8,256,176]{2,1,3,0:T(8,128)(2,1)} copy(bf16[16,8,256,176]{2,0,3,1:T(8,128)(2,1)} %bitcast.2) | data formatting | bytes 23068672 | tf_op jit(solution)/shard_map/all_to_all | solution.py:25
  563.3 18.0 %all_to_all.42 = bf16[16,2048,176]{1,2,0:T(8,128)(2,1)} reshape(bf16[16,8,256,176]{2,1,3,0:T(8,128)(2,1)} %copy.26) | data formatting | bytes 23068672 | tf_op jit(solution)/shard_map/all_to_all | solution.py:25
  581.2 0.0 all-to-all-done.2
  581.2 11.3 %copy.33 = bf16[16,176,8,256]{3,2,1,0:T(8,128)(2,1)} copy(bf16[16,176,8,256]{3,0,1,2:T(8,128)(2,1)} %bitcast.7) | data formatting | bytes 23068672 | tf_op jit(solution)/shard_map/all_to_all | solution.py:28
  592.5 18.0 %all_to_all.50 = bf16[16,176,2048]{2,1,0:T(8,128)(2,1)} reshape(bf16[16,176,8,256]{3,2,1,0:T(8,128)(2,1)} %copy.33) | data formatting | bytes 23068672 | tf_op jit(solution)/shard_map/all_to_all | solution.py:28
  610.5 0.7 copy.43
  (3 shorter events, 0.1 us)
Async XLA Ops:
  7.2 81.6 %all-reduce.3.cloned.1.call-start = ((), (), s32[]{:S(2)}) async-start(), calls=%async_computation.3 | async-start | bytes 540672 | tf_op jit(solution)/shard_map/psum | solution.py:8
  7.2 14.2 %copy-start = (f32[16,256,1408]{2,1,0:T(8,128)S(1)}, f32[16,256,1408]{2,1,0:T(8,128)}, u32[]{:S(2)}) copy-start(f32[16,256,1408]{2,1,0:T(8,128)} %param.6) | copy-start | bytes 69206016
  104.2 133.0 %all-to-all-start.1 = ((bf16[16,256,1408]{1,0,2:T(8,128)(2,1)}), bf16[16,256,1408]{1,0,2:T(8,128)(2,1)}, u32[]{:S(2)}, u32[]{:S(2)}) async-start(bf16[16,256,1408]{1,0,2:T(8,128)(2,1)} %divide_convert_fusion), calls=%async_computation.1 | async-start | bytes 23068672 | tf_op jit(solution)/shard_map/all_to_all | solution.py:26
  109.5 23.7 %copy-start.2 = (f32[16,1408]{1,0:T(8,128)S(1)}, f32[16,1408]{1,0:T(8,128)}, u32[]{:S(2)}) copy-start(f32[16,1408]{1,0:T(8,128)} %get-tuple-element.7) | copy-start | bytes 270340
  133.5 109.0 %copy-start.1 = (f32[16,1408]{1,0:T(8,128)S(1)}, f32[16,1408]{1,0:T(8,128)}, u32[]{:S(2)}) copy-start(f32[16,1408]{1,0:T(8,128)} %get-tuple-element.9) | copy-start | bytes 270340
  237.2 133.0 %all-to-all-start = ((bf16[16,256,1408]{1,0,2:T(8,128)(2,1)}), bf16[16,256,1408]{1,0,2:T(8,128)(2,1)}, u32[]{:S(2)}, u32[]{:S(2)}) async-start(bf16[16,256,1408]{1,0,2:T(8,128)(2,1)} %divide_convert_fusion.1), calls=%async_computation | async-start | bytes 23068672 | tf_op jit(solution)/shard_map/all_to_all | solution.py:25
  242.8 132.7 %copy-start.3 = (f32[256,16]{0,1:T(8,128)S(1)}, f32[256,16]{0,1:T(8,128)}, u32[]{:S(2)}) copy-start(f32[256,16]{0,1:T(8,128)} %param.8) | copy-start | bytes 49156
  242.8 132.7 %copy-start.4 = (f32[256]{0:T(256)S(1)}, f32[256]{0:T(256)}, u32[]{:S(2)}) copy-start(f32[256]{0:T(256)} %param.9) | copy-start | bytes 3076
  370.2 211.0 %all-to-all-start.2 = ((bf16[16,1408,256]{2,0,1:T(8,128)(2,1)}), bf16[16,1408,256]{2,0,1:T(8,128)(2,1)}, u32[]{:S(2)}, u32[]{:S(2)}) async-start(bf16[16,1408,256]{2,0,1:T(8,128)(2,1)} %fusion), calls=%async_computation.2 | async-start | bytes 23068672 | tf_op jit(solution)/shard_map/all_to_all | solution.py:28
Sparse Core Ops, SparseCore 0:
  32.6 56.1 all-reduce.2
where the time goes:
time: 621 us; the launch traced here: 618 us
  waiting for transfers between devices  217 us (35%)
  local copies, waits for them, and re-layouts  145 us (23%)
  blocking collectives  145 us (23%)
  other arithmetic  81.3 us (13%)
  starting transfers between devices  15.8 us (3%)
  between operations  14.2 us (2%)
    all_gather x1, blocking collectives, body(): row_router = lax.all_gather(part_router, 'fsdp', axis=0, tiled=True)  131 us
    all_to_all x1, waiting for transfers between devices, body(): lax.all_to_all(narrow_gate, 'fsdp', split_axis=2, concat_axis=1, tiled=True)  94.8 us
    all_to_all x1, waiting for transfers between devices, body(): lax.all_to_all(narrow_up, 'fsdp', split_axis=2, concat_axis=1, tiled=True)  89.5 us
    unnamed x13, local copies, waits for them, and re-layouts  53.2 us
    psum x1, waiting for transfers between devices, body(): lax.psum((jnp.sum(train_gate * train_gate, axis=1), jnp.sum(train_up * tr...  32.6 us
    convert_element_type x1, other arithmetic, body(): (train_down / jnp.expand_dims(scale_down, 2)).astype(jnp.bfloat16)  32.6 us
    all_to_all x2, local copies, waits for them, and re-layouts, body(): lax.all_to_all(narrow_up, 'fsdp', split_axis=2, concat_axis=1, tiled=True)  29.3 us
    all_to_all x2, local copies, waits for them, and re-layouts, body(): lax.all_to_all(narrow_gate, 'fsdp', split_axis=2, concat_axis=1, tiled=True)  29.3 us
  transfers between devices with their start and end apart: 4, of which 3 were waited for; matrix products, arithmetic and copies ran while one was open for 19% of the time, Pallas kernels for 0%

commit v1 on v0

--- a/solution.py
+++ b/solution.py
@@ -2,6 +2,15 @@
 import jax.numpy as jnp
 from jax import lax
 from jax.sharding import PartitionSpec as P
+
+
+def _connect_lines(patch):
+    return jnp.concatenate(
+        lax.all_to_all(
+            jnp.stack(jnp.split(patch, lax.axis_size("fsdp"), axis=1), axis=0), "fsdp", 0, 0
+        ),
+        axis=2,
+    )
 
 
 def body(train_gate, train_up, train_down, router_weight, router_gain):
@@ -25,7 +34,7 @@
         lax.all_to_all(narrow_gate, "fsdp", split_axis=2, concat_axis=1, tiled=True),
         lax.all_to_all(narrow_up, "fsdp", split_axis=2, concat_axis=1, tiled=True),
     )
-    ready_down = lax.all_to_all(narrow_down, "fsdp", split_axis=1, concat_axis=2, tiled=True)
+    ready_down = _connect_lines(narrow_down)
     scale_gate = lax.dynamic_slice_in_dim(
         scale_gate, lax.axis_index("fsdp") * ready_gate.shape[2], ready_gate.shape[2], axis=1
     )

time: 621 us -> 601 us (0.968)
  other arithmetic: 81.3 us -> 58.4 us
  waiting for transfers between devices: 217 us -> 230 us
  local copies, waits for them, and re-layouts: 145 us -> 135 us
    all_to_all x2 -> x0, local copies, waits for them, and re-layouts: 29.3 us -> none  [body(): lax.all_to_all(narrow_down, 'fsdp', split_axis=1, concat_axis=2, tiled=True)]
    convert_element_type x1, other arithmetic: 32.6 us -> 9.8 us  [body(): (train_down / jnp.expand_dims(scale_down, 2)).astype(jnp.bfloat16)]
    all_to_all x1, waiting for transfers between devices: 89.5 us -> 108 us  [body(): lax.all_to_all(narrow_up, 'fsdp', split_axis=2, concat_axis=1, tiled=True)]
    reshape x0 -> x1, local copies, waits for them, and re-layouts: none -> 10 us  [_connect_lines(): jnp.concatenate(lax.all_to_all(jnp.stack(jnp.split(patch, lax.axis_size('...]
    unnamed x13 -> x20, local copies, waits for them, and re-layouts: 53.2 us -> 61.6 us
  transfers between devices with their start and end apart: 4 -> 4, of which waited for: 3 -> 3; matrix products, arithmetic and copies ran while one was open for 19% -> 18% of each run, Pallas kernels for 0% -> 0%
where the time goes in v1:
time: 601 us; the launch traced here: 599 us
  waiting for transfers between devices  230 us (38%)
  blocking collectives  145 us (24%)
  local copies, waits for them, and re-layouts  135 us (22%)
  other arithmetic  58.4 us (10%)
  starting transfers between devices  15.8 us (3%)
  between operations  14.2 us (2%)
    all_gather x1, blocking collectives, body(): row_router = lax.all_gather(part_router, 'fsdp', axis=0, tiled=True)  131 us
    all_to_all x1, waiting for transfers between devices, body(): lax.all_to_all(narrow_up, 'fsdp', split_axis=2, concat_axis=1, tiled=True)  108 us
    all_to_all x1, waiting for transfers between devices, body(): lax.all_to_all(narrow_gate, 'fsdp', split_axis=2, concat_axis=1, tiled=True)  89.5 us
    unnamed x20, local copies, waits for them, and re-layouts  61.6 us
    psum x1, waiting for transfers between devices, body(): lax.psum((jnp.sum(train_gate * train_gate, axis=1), jnp.sum(train_up * tr...  32.6 us
    all_to_all x2, local copies, waits for them, and re-layouts, body(): lax.all_to_all(narrow_gate, 'fsdp', split_axis=2, concat_axis=1, tiled=True)  29.3 us
    all_to_all x2, local copies, waits for them, and re-layouts, body(): lax.all_to_all(narrow_up, 'fsdp', split_axis=2, concat_axis=1, tiled=True)  29.3 us
    convert_element_type x1, other arithmetic, body(): (train_gate / jnp.expand_dims(scale_gate, 1)).astype(jnp.bfloat16)  14.2 us
  transfers between devices with their start and end apart: 4, of which 3 were waited for; matrix products, arithmetic and copies ran while one was open for 18% of the time, Pallas kernels for 0%

profile of v1, /device:TPU:0, one launch (start us, length us, event | category | flops | bytes accessed | tf_op | source)
XLA Modules:
  0.0 598.6 jit_solution(13294843355749085687)
XLA Ops:
  7.2 0.0 all-reduce.3.cloned.1.call-start
  7.2 0.0 copy-start
  7.2 9.2 %multiply_reduce_fusion = f32[16,1408]{1,0:T(8,128)} fusion(f32[16,1408,256]{2,1,0:T(8,128)} %param.7), kind=kLoop, calls=%fused_computation.1 | loop fusion | flops 11511808 | bytes 23158784 | tf_op jit(solution)/shard_map/reduce_sum | solution.py:21
  16.4 5.0 copy-done
  21.4 11.0 %multiply_reduce_fusion.1 = (f32[16,1408]{1,0:T(8,128)}, f32[16,1408]{1,0:T(8,128)}) fusion(f32[16,256,1408]{2,1,0:T(8,128)} %param.6, f32[16,256,1408]{2,1,0:T(8,128)S(1)} %copy-done), kind=kLoop, calls=%fused_computation.3 | loop fusion | flops 23023616 | bytes 46317568 | tf_op jit(solution)/shard_map/reduce_sum | solution.py:20
  32.4 0.0 all-reduce.3.cloned.1.call-update
  32.5 23.7 %copy.24 = f32[16,256,1408]{1,0,2:T(8,128)} copy(f32[16,256,1408]{2,1,0:T(8,128)} %param.5) | data formatting | bytes 46137344 | tf_op args[0]
  56.2 32.6 %all-reduce.3.cloned.1.call-done = (f32[16,1408]{1,0:T(8,128)}, f32[16,1408]{1,0:T(8,128)}, f32[16,1408]{1,0:T(8,128)}) async-done(((f32[16,1408]{1,0:T(8,128)}, f32[16,1408]{1,0:T(8,128)}, f32[16,1408]{1,0:T(8,128)}), (f32[16,1408]{1,0:T(8,128)}, f32[16,1408]{1,0:T(8,128)}, f32[16,1408]{1,0:T(8,128)})) %all-reduce.3.cloned.1.call-update) | async-done | bytes 270352 | tf_op jit(solution)/shard_map/psum | solution.py:17
  88.8 0.9 sqrt.9
  89.7 0.3 copy.23
  90.0 14.2 %divide_convert_fusion.2 = bf16[16,256,1408]{1,0,2:T(8,128)(2,1)} fusion(f32[16,256,1408]{1,0,2:T(8,128)} %copy.24, f32[16,1408]{0,1:T(8,128)S(1)} %copy.23), kind=kLoop, calls=%fused_computation.4 | loop fusion | flops 11534336 | bytes 34693120 | tf_op jit(solution)/shard_map/convert_element_type | solution.py:29
  104.2 5.2 all-to-all-start
  109.4 0.0 copy-start.2
  109.4 23.7 %copy.28 = f32[16,256,1408]{1,0,2:T(8,128)} copy(f32[16,256,1408]{2,1,0:T(8,128)} %param.6) | data formatting | bytes 46137344 | tf_op args[1]
  133.1 0.0 copy-done.2
  133.2 0.3 copy.27
  133.4 14.2 %divide_convert_fusion.1 = bf16[16,256,1408]{1,0,2:T(8,128)(2,1)} fusion(f32[16,256,1408]{1,0,2:T(8,128)} %copy.28, f32[16,1408]{0,1:T(8,128)S(1)} %copy.27), kind=kLoop, calls=%fused_computation.2 | loop fusion | flops 11534336 | bytes 34693120 | tf_op jit(solution)/shard_map/convert_element_type | solution.py:30
  147.7 0.0 copy-start.1
  147.7 89.5 %all-to-all-done = bf16[16,256,1408]{1,0,2:T(8,128)(2,1)} async-done(((bf16[16,256,1408]{1,0,2:T(8,128)(2,1)}), bf16[16,256,1408]{1,0,2:T(8,128)(2,1)}, u32[]{:S(2)}, u32[]{:S(2)}) %all-to-all-start) | async-done | bytes 11534368 | tf_op jit(solution)/shard_map/all_to_all | solution.py:34
  237.2 5.3 all-to-all-start.1
  242.4 0.0 copy-done.1
  242.5 9.8 %divide_convert_fusion = bf16[16,1408,256]{2,1,0:T(8,128)(2,1)S(1)} fusion(f32[16,1408,256]{2,1,0:T(8,128)} %param.7, f32[16,1408]{1,0:T(8,128)S(1)} %sqrt.11), kind=kLoop, calls=%fused_computation | loop fusion | flops 11534336 | bytes 34693120 | tf_op jit(solution)/shard_map/convert_element_type | solution.py:31
  252.3 1.2 fusion.7
  253.5 1.2 fusion.6
  254.7 1.2 fusion.5
  255.9 1.2 fusion.4
  257.1 1.2 fusion.3
  258.3 1.2 fusion.2
  259.5 1.2 fusion.1
  260.7 1.2 fusion
  261.9 0.0 copy-start.3
  261.9 0.0 copy-start.4
  261.9 108.3 %all-to-all-done.1 = bf16[16,256,1408]{1,0,2:T(8,128)(2,1)} async-done(((bf16[16,256,1408]{1,0,2:T(8,128)(2,1)}), bf16[16,256,1408]{1,0,2:T(8,128)(2,1)}, u32[]{:S(2)}, u32[]{:S(2)}) %all-to-all-start.1) | async-done | bytes 11534368 | tf_op jit(solution)/shard_map/all_to_all | solution.py:35
  370.2 5.3 all-to-all-start.2
  375.5 0.0 copy-done.3
  375.5 0.0 copy-done.4
  375.5 130.9 %all_gather.6 = bf16[2048,16]{0,1:T(8,128)(2,1)S(1)} all-gather(bf16[256,16]{0,1:T(8,128)(2,1)S(1)} %multiply_convert_fusion), channel_id=1, replica_groups=mesh['ep'=4,'fsdp'=8] {'fsdp'}, dimensions={0}, use_global_device_ids=true | all-gather | bytes 73728 | tf_op jit(solution)/shard_map/all_gather | solution.py:48
  506.4 14.0 %all_gather.7 = bf16[2048,64]{0,1:T(8,128)(2,1)S(1)} all-gather(bf16[2048,16]{0,1:T(8,128)(2,1)S(1)} %all_gather.6), channel_id=1, replica_groups=mesh['ep'=4,'fsdp'=8] {'ep'}, dimensions={1}, use_global_device_ids=true | all-gather | bytes 327680 | tf_op jit(solution)/shard_map/all_gather | solution.py:49
  520.4 0.7 constant_dynamic-slice_fusion.2
  521.1 0.7 constant_dynamic-slice_fusion.1
  521.8 0.7 constant_dynamic-slice_fusion
  522.4 11.3 %copy.26 = bf16[16,8,256,176]{2,1,3,0:T(8,128)(2,1)} copy(bf16[16,8,256,176]{2,0,3,1:T(8,128)(2,1)} %bitcast.2) | data formatting | bytes 23068672 | tf_op jit(solution)/shard_map/all_to_all | solution.py:34
  533.8 18.0 %all_to_all.32 = bf16[16,2048,176]{1,2,0:T(8,128)(2,1)} reshape(bf16[16,8,256,176]{2,1,3,0:T(8,128)(2,1)} %copy.26) | data formatting | bytes 23068672 | tf_op jit(solution)/shard_map/all_to_all | solution.py:34
  551.7 11.3 %copy.30 = bf16[16,8,256,176]{2,1,3,0:T(8,128)(2,1)} copy(bf16[16,8,256,176]{2,0,3,1:T(8,128)(2,1)} %bitcast.5) | data formatting | bytes 23068672 | tf_op jit(solution)/shard_map/all_to_all | solution.py:35
  563.1 18.0 %all_to_all.36 = bf16[16,2048,176]{1,2,0:T(8,128)(2,1)} reshape(bf16[16,8,256,176]{2,1,3,0:T(8,128)(2,1)} %copy.30) | data formatting | bytes 23068672 | tf_op jit(solution)/shard_map/all_to_all | solution.py:35
  581.0 0.0 all-to-all-done.2
  581.0 10.0 %copy.34 = bf16[8,16,22,8,256]{4,3,0,2,1:T(8,128)(2,1)} copy(bf16[8,16,22,8,256]{4,3,2,1,0:T(8,128)(2,1)} %bitcast.15) | data formatting | bytes 23068672 | tf_op jit(solution)/shard_map/reshape | solution.py:8
  591.0 0.7 copy.46
  (3 shorter events, 0.1 us)
Async XLA Ops:
  7.2 81.6 %all-reduce.3.cloned.1.call-start = ((), (), s32[]{:S(2)}) async-start(), calls=%async_computation.3 | async-start | bytes 540672 | tf_op jit(solution)/shard_map/psum | solution.py:17
  7.2 14.2 %copy-start = (f32[16,256,1408]{2,1,0:T(8,128)S(1)}, f32[16,256,1408]{2,1,0:T(8,128)}, u32[]{:S(2)}) copy-start(f32[16,256,1408]{2,1,0:T(8,128)} %param.5) | copy-start | bytes 69206016
  104.2 133.0 %all-to-all-start = ((bf16[16,256,1408]{1,0,2:T(8,128)(2,1)}), bf16[16,256,1408]{1,0,2:T(8,128)(2,1)}, u32[]{:S(2)}, u32[]{:S(2)}) async-start(bf16[16,256,1408]{1,0,2:T(8,128)(2,1)} %divide_convert_fusion.2), calls=%async_computation | async-start | bytes 23068672 | tf_op jit(solution)/shard_map/all_to_all | solution.py:34
  109.4 23.7 %copy-start.2 = (f32[16,1408]{1,0:T(8,128)S(1)}, f32[16,1408]{1,0:T(8,128)}, u32[]{:S(2)}) copy-start(f32[16,1408]{1,0:T(8,128)} %get-tuple-element.8) | copy-start | bytes 270340
  147.7 94.8 %copy-start.1 = (f32[16,1408]{1,0:T(8,128)S(1)}, f32[16,1408]{1,0:T(8,128)}, u32[]{:S(2)}) copy-start(f32[16,1408]{1,0:T(8,128)} %get-tuple-element.9) | copy-start | bytes 270340
  237.2 133.0 %all-to-all-start.1 = ((bf16[16,256,1408]{1,0,2:T(8,128)(2,1)}), bf16[16,256,1408]{1,0,2:T(8,128)(2,1)}, u32[]{:S(2)}, u32[]{:S(2)}) async-start(bf16[16,256,1408]{1,0,2:T(8,128)(2,1)} %divide_convert_fusion.1), calls=%async_computation.1 | async-start | bytes 23068672 | tf_op jit(solution)/shard_map/all_to_all | solution.py:35
  261.9 113.6 %copy-start.3 = (f32[256,16]{0,1:T(8,128)S(1)}, f32[256,16]{0,1:T(8,128)}, u32[]{:S(2)}) copy-start(f32[256,16]{0,1:T(8,128)} %param.8) | copy-start | bytes 49156
  261.9 113.6 %copy-start.4 = (f32[256]{0:T(256)S(1)}, f32[256]{0:T(256)}, u32[]{:S(2)}) copy-start(f32[256]{0:T(256)} %param.9) | copy-start | bytes 3076
  370.2 210.8 %all-to-all-start.2 = ((bf16[8,16,176,256]{3,2,1,0:T(8,128)(2,1)}), bf16[8,16,176,256]{3,2,1,0:T(8,128)(2,1)}, u32[]{:S(2)}, u32[]{:S(2)}) async-start(bf16[8,16,176,256]{3,2,1,0:T(8,128)(2,1)} %fusion), calls=%async_computation.2 | async-start | bytes 23068672 | tf_op jit(solution)/shard_map/all_to_all | solution.py:9
Sparse Core Ops, SparseCore 0:
  32.6 56.1 all-reduce.2
